TPU v7x, 32 devices: a whole 2x2x4 slice. The times are simulated.
32 devices in a mesh: ia: 4 (over y, x), ja: 4 (over z), col: 2 (over core).
Axes of the slice: x: 2, y: 2, z: 4, core: 2. Of those that a mesh axis runs over, the one named last changes fastest.
Arguments:
- pair_rep: bfloat16 [512, 512, 128], P('ia', 'ja'), may hold values from -6 to 6
- norm_gain: float32 [128], replicated, may hold values from 0.1 to 1.9
- weights: bfloat16 [4, 128, 128], P(None, None, 'col'), may hold values from -0.5 to 0.5
- residue_mask: int32 [512], replicated, may hold values 0 or 1
- product_grad: bfloat16 [512, 128, 512], P('ia', 'col', 'ja'), may hold values from -1 to 1
Outputs:
- pair_grad: bfloat16 [512, 512, 128], P('ia', 'ja')
- weight_grads: float32 [4, 128, 128], P(None, None, 'col')
All inputs are finite; a program needn't handle non-finite values.
Results may differ from a plain program's by a relative error of at most 0.0067.
Values may be sent and summed in bfloat16 or wider, within the bound.
A program may use at most 128 MiB of HBM per device.

v0:
```python
import jax
import jax.numpy as jnp
from jax import lax
from jax.sharding import PartitionSpec as P

CLIP_LIMIT = 64.0


def gate_terms(incoming, linear, gate_pre, pair_valid):
    sigmoid_gate = jax.nn.sigmoid(gate_pre)
    through = incoming * pair_valid
    return (through * sigmoid_gate, through * linear * sigmoid_gate * (1.0 - sigmoid_gate))


def on_device(pair_rep, norm_gain, weights, residue_mask, product_grad):
    row_count = pair_rep.shape[0]
    col_count = pair_rep.shape[1]
    row_first = lax.axis_index("ia") * row_count
    col_first = lax.axis_index("ja") * col_count
    validity = residue_mask.astype(jnp.float32)
    row_valid = lax.dynamic_slice_in_dim(validity, row_first, row_count)
    col_valid = lax.dynamic_slice_in_dim(validity, col_first, col_count)
    pair_valid = row_valid[:, None, None] * col_valid[None, None, :]
    floats = pair_rep.astype(jnp.float32)
    centred = floats - jnp.mean(floats, axis=-1, keepdims=True)
    inv_std = lax.rsqrt(jnp.mean(centred * centred, axis=-1, keepdims=True) + 1e-05)
    unit_rows = centred * inv_std
    normed = (unit_rows * norm_gain).astype(jnp.bfloat16)
    projected = jnp.einsum("ikd,wdc->wick", normed, weights, preferred_element_type=jnp.float32)
    left_side = (pair_valid * jax.nn.sigmoid(projected[1]) * projected[0]).astype(jnp.bfloat16)
    right_side = (pair_valid * jax.nn.sigmoid(projected[3]) * projected[2]).astype(jnp.bfloat16)
    row_panel = lax.all_gather(product_grad, "ja", axis=2, tiled=True)
    panel_part = row_panel
    grad_left = jnp.einsum(
        "icj,jck->ick",
        panel_part,
        lax.all_gather(right_side, "ia", axis=0, tiled=True),
        preferred_element_type=jnp.float32,
    )
    panel_part = row_panel
    grad_right = lax.psum_scatter(
        jnp.einsum("icj,ick->jck", panel_part, left_side, preferred_element_type=jnp.float32),
        "ia",
        scatter_dimension=0,
        tiled=True,
    )
    lin_a, gate_a = gate_terms(grad_left, projected[0], projected[1], pair_valid)
    lin_b, gate_b = gate_terms(grad_right, projected[2], projected[3], pair_valid)
    proj_grads = jnp.stack([lin_a, gate_a, lin_b, gate_b]).astype(jnp.bfloat16)
    grad_part = jnp.einsum("ikd,wick->wdc", normed, proj_grads, preferred_element_type=jnp.float32)
    input_part = jnp.einsum(
        "wick,wdc->ikd", proj_grads, weights, preferred_element_type=jnp.float32
    )
    normed_grad = lax.psum(input_part, "col")
    scaled = normed_grad * norm_gain
    pair_grad = inv_std * (
        scaled
        - jnp.mean(scaled, axis=-1, keepdims=True)
        - unit_rows * jnp.mean(scaled * unit_rows, axis=-1, keepdims=True)
    )
    summed = lax.psum(grad_part, ("ia", "ja"))
    squares = lax.psum(jnp.sum(summed * summed), "col")
    factor = jnp.minimum(1.0, CLIP_LIMIT * lax.rsqrt(squares + 1e-06))
    weight_grads = summed * factor
    return (pair_grad.astype(jnp.bfloat16), weight_grads)


def solution(mesh):
    placed = (P("ia", "ja", None), P(), P(None, None, "col"), P(), P("ia", "col", "ja"))
    return jax.shard_map(
        on_device,
        mesh=mesh,
        in_specs=placed,
        out_specs=(P("ia", "ja", None), P(None, None, "col")),
        check_vma=False,
    )
```

profile of v0, /device:TPU:0, one launch (start us, length us, event | category | flops | bytes accessed | tf_op | source)
XLA Modules:
  0.0 660.3 jit_solution(14896707460684824877)
XLA Ops:
  7.2 0.0 copy-start
  7.2 0.0 copy-start.10
  7.2 0.0 all-gather.5.cloned.1.call-start
  7.2 4.3 copy.18
  11.5 0.0 all-gather.5.cloned.1.call-update
  11.5 0.0 all-gather.3.cloned.1.call-start
  11.6 0.0 copy-done.10
  11.6 0.0 copy-start.2
  11.6 0.1 fusion.41
  11.7 0.1 broadcast_multiply_fusion.1
  11.8 0.0 copy-start.9
  11.8 3.5 convert_reduce_fusion
  15.3 0.0 copy-done.2
  15.3 4.8 fusion.10
  20.1 0.0 copy-done
  20.2 0.0 copy-done.9
  20.2 4.7 convolution_bitcast_fusion
  24.9 0.0 copy-start.1
  24.9 5.9 copy-done.1
  30.8 2.6 multiply_convert_fusion.5
  33.4 0.0 all-gather.3.cloned.1.call-update
  33.4 0.5 reduce-scatter.2.cloned.1.call-start
  33.9 129.6 %all-gather.5.cloned.1.call-done = bf16[128,64,512]{2,0,1:T(8,128)(2,1)} async-done(((bf16[128,64,128]{2,0,1:T(8,128)(2,1)}), bf16[128,64,512]{2,0,1:T(8,128)(2,1)}) %all-gather.5.cloned.1.call-update) | async-done | bytes 8388624 | tf_op jit(solution)/shard_map/all_gather | solution.py:32
  163.5 87.5 %all-gather.3.cloned.1.call-done = bf16[512,64,128]{2,1,0:T(8,128)(2,1)} async-done(((bf16[128,64,128]{2,1,0:T(8,128)(2,1)}), bf16[512,64,128]{2,1,0:T(8,128)(2,1)}) %all-gather.3.cloned.1.call-update) | async-done | bytes 8388624 | tf_op jit(solution)/shard_map/all_gather | solution.py:37
  251.0 25.2 %fusion.11 = f32[64,128,128]{2,1,0:T(8,128)} fusion(bf16[128,64,512]{2,0,1:T(8,128)(2,1)} %all-gather.5.cloned.1.call-done, bf16[512,64,128]{2,1,0:T(8,128)(2,1)} %all-gather.3.cloned.1.call-done), kind=kOutput, calls=%fused_computation.15 | convolution fusion | flops 1073741824 | bytes 20971520 | tf_op jit(solution)/shard_map/icj,jck->ick/dot_general | solution.py:34
  276.2 5.4 copy.20
  281.6 6.8 %fusion.28 = (bf16[1,128,64,128]{3,2,1,0:T(8,128)(2,1)S(1)}, bf16[1,128,64,128]{3,2,1,0:T(8,128)(2,1)}, bf16[128,64,128]{2,1,0:T(8,128)(2,1)S(1)}) fusion(f32[64,128,128]{1,0,2:T(8,128)} %copy.20, f32[128,128]{1,0:T(8,128)S(1)} %broadcast_multiply_fusion.1, f32[4,128,64,128]{3,2,0,1:T(8,128)} %copy-done.1), kind=kLoop, calls=%fused_computation.43 | loop fusion | flops 14680064 | bytes 18939904 | tf_op jit(solution)/shard_map/stack | solution.py:49
  288.5 14.1 %fusion.32 = f32[64,128,512]{2,1,0:T(8,128)} fusion(bf16[128,64,512]{2,0,1:T(8,128)(2,1)} %all-gather.5.cloned.1.call-done, bf16[128,64,128]{2,1,0:T(8,128)(2,1)S(1)} %get-tuple-element.8), kind=kOutput, calls=%fused_computation.47 | convolution fusion | flops 1073741824 | bytes 27262976 | tf_op jit(solution)/shard_map/icj,ick->jck/dot_general | solution.py:42
  302.6 16.6 %copy.23 = f32[64,128,512]{1,0,2:T(8,128)} copy(f32[64,128,512]{2,1,0:T(8,128)} %fusion.32) | data formatting | bytes 33554432 | tf_op jit(solution)/shard_map/icj,ick->jck/dot_general | solution.py:42
  319.2 0.0 reduce-scatter.2.cloned.1.call-update
  319.2 0.0 all-reduce.5.cloned.1.call-start
  319.2 153.8 %reduce-scatter.2.cloned.1.call-done = f32[128,64,128]{2,1,0:T(8,128)} async-done(((f32[512,64,128]{2,1,0:T(8,128)}), f32[128,64,128]{2,1,0:T(8,128)}) %reduce-scatter.2.cloned.1.call-update) | async-done | bytes 4194320 | tf_op jit(solution)/shard_map/reduce_scatter | solution.py:41
  473.1 6.0 fusion.30
  479.1 0.0 copy-start.7
  479.2 1.3 copy-done.7
  480.4 0.7 copy-done.8
  481.1 5.4 fusion.34
  486.5 0.0 all-reduce.5.cloned.1.call-update
  486.6 0.0 all-reduce.3.cloned.1.call-start
  486.6 6.5 convolution_bitcast_fusion.1
  493.1 0.0 all-reduce.3.cloned.1.call-update
  493.1 99.0 %all-reduce.5.cloned.1.call-done = f32[4,128,64]{1,2,0:T(8,128)} async-done(((f32[4,128,64]{1,2,0:T(8,128)}), f32[4,128,64]{1,2,0:T(8,128)}) %all-reduce.5.cloned.1.call-update) | async-done | bytes 131088 | tf_op jit(solution)/shard_map/psum | solution.py:61
  592.1 1.5 multiply_reduce_fusion.1
  593.7 3.1 psum.23
  597.4 1.6 broadcast_multiply_fusion
  599.0 32.2 %all-reduce.3.cloned.1.call-done = f32[128,128,128]{2,1,0:T(8,128)} async-done(((f32[128,128,128]{2,1,0:T(8,128)}), f32[128,128,128]{2,1,0:T(8,128)}) %all-reduce.3.cloned.1.call-update) | async-done | bytes 8388624 | tf_op jit(solution)/shard_map/psum | solution.py:54
  631.2 11.6 %multiply_reduce_fusion = (f32[128,128]{1,0:T(8,128)S(1)}, f32[128,128]{1,0:T(8,128)S(1)}) fusion(f32[128,128,128]{2,1,0:T(8,128)} %all-reduce.3.cloned.1.call-done, f32[128]{0:T(128)S(1)} %copy-done.9, f32[128,128]{1,0:T(8,128)S(1)} %add_rsqrt_fusion, f32[128,128]{1,0:T(8,128)S(1)} %broadcast_multiply_fusion.4, bf16[128,128,128]{2,1,0:T(8,128)(2,1)} %param.5), kind=kLoop, calls=%fused_computation.17 | loop fusion | flops 14647296 | bytes 12845568 | tf_op jit(solution)/shard_map/reduce_sum | solution.py:58
  642.8 10.7 %fusion.9 = bf16[128,128,128]{2,1,0:T(8,128)(2,1)} fusion(bf16[128,128,128]{2,1,0:T(8,128)(2,1)S(1)} %copy-done.4, f32[128,128,128]{2,1,0:T(8,128)S(1)} %copy-done.5, f32[128,128]{1,0:T(8,128)S(1)} %get-tuple-element.11, f32[128,128]{1,0:T(8,128)S(1)} %get-tuple-element.12, f32[128]{0:T(128)S(1)} %copy-done.9, f32[128,128]{1,0:T(8,128)S(1)} %add_rsqrt_fusion, ...), kind=kLoop, calls=%fused_computation.12 | loop fusion | flops 18874368 | bytes 17039872 | tf_op jit(solution)/shard_map/convert_element_type | solution.py:65
  (13 shorter events, 0.1 us)
Async XLA Ops:
  7.2 13.0 %copy-start = (bf16[4,128,64]{1,2,0:T(8,128)(2,1)S(1)}, bf16[4,128,64]{1,2,0:T(8,128)(2,1)}, u32[]{:S(2)}) copy-start(bf16[4,128,64]{1,2,0:T(8,128)(2,1)} %param.7) | copy-start | bytes 196612
  7.2 4.4 copy-start.10
  7.2 156.3 %all-gather.5.cloned.1.call-start = ((), (), s32[]{:S(2)}) async-start(), calls=%async_computation.2 | async-start | bytes 10485760 | tf_op jit(solution)/shard_map/all_gather | solution.py:32
  11.5 239.5 %all-gather.3.cloned.1.call-start = ((), (), s32[]{:S(2)}) async-start(), calls=%async_computation.1 | async-start | bytes 10485760 | tf_op jit(solution)/shard_map/all_gather | solution.py:37
  11.6 3.7 copy-start.2
  11.8 8.4 %copy-start.9 = (f32[128]{0:T(128)S(1)}, f32[128]{0:T(128)}, u32[]{:S(2)}) copy-start(f32[128]{0:T(128)} %param.6) | copy-start | bytes 1540
  24.9 5.9 copy-start.1
  33.4 439.6 %reduce-scatter.2.cloned.1.call-start = ((), (), s32[]{:S(2)}) async-start(), calls=%async_computation.3 | async-start | bytes 20971520 | tf_op jit(solution)/shard_map/reduce_scatter | solution.py:41
  319.2 272.9 %all-reduce.5.cloned.1.call-start = ((), (), s32[]{:S(2)}) async-start(), calls=%async_computation.5 | async-start | bytes 262144 | tf_op jit(solution)/shard_map/psum | solution.py:61
  473.1 8.0 %copy-start.3 = (bf16[128,128,128]{2,1,0:T(8,128)(2,1)S(1)}, bf16[128,128,128]{2,1,0:T(8,128)(2,1)}, u32[]{:S(2)}) copy-start(bf16[128,128,128]{2,1,0:T(8,128)(2,1)} %param.5) | copy-start | bytes 12582916
  473.1 8.0 %copy-start.6 = (bf16[1,128,64,128]{3,2,1,0:T(8,128)(2,1)S(1)}, bf16[1,128,64,128]{3,2,1,0:T(8,128)(2,1)}, u32[]{:S(2)}) copy-start(bf16[1,128,64,128]{3,2,1,0:T(8,128)(2,1)} %get-tuple-element.5) | copy-start | bytes 6291460
  479.1 1.3 copy-start.7
  479.1 2.0 copy-start.8
  486.6 144.6 %all-reduce.3.cloned.1.call-start = ((), (), s32[]{:S(2)}) async-start(), calls=%async_computation.4 | async-start | bytes 16777216 | tf_op jit(solution)/shard_map/psum | solution.py:54
  631.2 11.6 %copy-start.4 = (bf16[128,128,128]{2,1,0:T(8,128)(2,1)S(1)}, bf16[128,128,128]{2,1,0:T(8,128)(2,1)}, u32[]{:S(2)}) copy-start(bf16[128,128,128]{2,1,0:T(8,128)(2,1)} %param.5) | copy-start | bytes 12582916
  631.2 11.6 %copy-start.5 = (f32[128,128,128]{2,1,0:T(8,128)S(1)}, f32[128,128,128]{2,1,0:T(8,128)}, u32[]{:S(2)}) copy-start(f32[128,128,128]{2,1,0:T(8,128)} %all-reduce.3.cloned.1.call-done) | copy-start | bytes 25165828
Sparse Core Ops, SparseCore 0:
  11.6 151.8 all-gather.4
  165.4 85.6 all-gather.2
  319.3 153.7 reduce-scatter.1
  486.7 105.3 all-reduce.4
  594.4 36.6 all-reduce.2
where the time goes:
time: 668 us; the launch traced here: 660 us
  waiting for transfers between devices  502 us (75%)
  matrix products  55.9 us (8%)
  other arithmetic  49.3 us (7%)
  local copies, waits for them, and re-layouts  34.2 us (5%)
  between operations  14.9 us (2%)
    reduce_scatter x1, waiting for transfers between devices, on_device(): lax.psum_scatter(jnp.einsum('icj,ick->jck', panel_part, left_side, prefer...  154 us
    all_gather x1, waiting for transfers between devices, on_device(): row_panel = lax.all_gather(product_grad, 'ja', axis=2, tiled=True)  130 us
    psum x1, waiting for transfers between devices, on_device(): summed = lax.psum(grad_part, ('ia', 'ja'))  99 us
    all_gather x1, waiting for transfers between devices, on_device(): lax.all_gather(right_side, 'ia', axis=0, tiled=True)  87.5 us
    psum x1, waiting for transfers between devices, on_device(): normed_grad = lax.psum(input_part, 'col')  32.2 us
    dot_general x1, matrix products, on_device(): jnp.einsum('icj,jck->ick', panel_part, lax.all_gather(right_side, 'ia', a...  25.2 us
    dot_general x1, local copies, waits for them, and re-layouts, on_device(): jnp.einsum('icj,ick->jck', panel_part, left_side, preferred_element_type=...  16.6 us
    dot_general x1, matrix products, on_device(): jnp.einsum('icj,ick->jck', panel_part, left_side, preferred_element_type=...  14.1 us
  transfers between devices with their start and end apart: 5, of which 5 were waited for; matrix products, arithmetic and copies ran while one was open for 4% of the time, Pallas kernels for 0%

commit v1 on v0

--- a/solution.py
+++ b/solution.py
@@ -31,12 +31,38 @@
     right_side = (pair_valid * jax.nn.sigmoid(projected[3]) * projected[2]).astype(jnp.bfloat16)
     row_panel = lax.all_gather(product_grad, "ja", axis=2, tiled=True)
     panel_part = row_panel
-    grad_left = jnp.einsum(
+    peers, here, span = (lax.axis_size("ia"), lax.axis_index("ia"), right_side.shape[0])
+    ahead = [(i, (i + 1) % peers) for i in range(peers)]
+    left = [(i, (i - 1) % peers) for i in range(peers)]
+    halfway = peers // 2
+    from_left = from_right = right_side
+    so_far = jnp.einsum(
         "icj,jck->ick",
-        panel_part,
-        lax.all_gather(right_side, "ia", axis=0, tiled=True),
+        lax.dynamic_slice_in_dim(panel_part, here * span, right_side.shape[0], axis=2),
+        right_side,
         preferred_element_type=jnp.float32,
     )
+    for step in range(1, halfway + 1):
+        from_left = lax.ppermute(from_left, "ia", ahead)
+        if step < peers - halfway:
+            from_right = lax.ppermute(from_right, "ia", left)
+            so_far = so_far + jnp.einsum(
+                "icj,jck->ick",
+                lax.dynamic_slice_in_dim(
+                    panel_part, (here + step) % peers * span, from_right.shape[0], axis=2
+                ),
+                from_right,
+                preferred_element_type=jnp.float32,
+            )
+        so_far = so_far + jnp.einsum(
+            "icj,jck->ick",
+            lax.dynamic_slice_in_dim(
+                panel_part, (here - step) % peers * span, from_left.shape[0], axis=2
+            ),
+            from_left,
+            preferred_element_type=jnp.float32,
+        )
+    grad_left = so_far
     panel_part = row_panel
     grad_right = lax.psum_scatter(
         jnp.einsum("icj,ick->jck", panel_part, left_side, preferred_element_type=jnp.float32),

time: 668 us -> 606 us (0.907)
  waiting for transfers between devices: 502 us -> 409 us
  local copies, waits for them, and re-layouts: 34.2 us -> 51.1 us
  other arithmetic: 49.3 us -> 57.8 us
    all_gather x1, waiting for transfers between devices: 130 us -> 32 us  [on_device(): row_panel = lax.all_gather(product_grad, 'ja', axis=2, tiled=True)]
    ppermute x0 -> x3, waiting for transfers between devices: none -> 93 us  [the longest x2 93 us: on_device(): from_left = lax.ppermute(from_left, 'ia', ahead)]
    all_gather x1 -> x0, waiting for transfers between devices: 87.5 us -> none  [on_device(): lax.all_gather(right_side, 'ia', axis=0, tiled=True)]
    dot_general x1 -> x4, local copies, waits for them, and re-layouts: 5.42 us -> 21.6 us  [the longest x2 10.8 us: on_device(): jnp.einsum('icj,jck->ick', lax.dynamic_slice_in_dim(panel_part, (here - s...]
    another operation x2, other arithmetic: 12.9 us -> 22.7 us  [on_device(): proj_grads = jnp.stack([lin_a, gate_a, lin_b, gate_b]).astype(jnp.bfloat16)]
    dot_general x1 -> x4, matrix products: 25.2 us -> 24.7 us  [the longest x2 12.6 us: on_device(): jnp.einsum('icj,jck->ick', lax.dynamic_slice_in_dim(panel_part, (here - s...]
  transfers between devices with their start and end apart: 5 -> 7, of which waited for: 5 -> 6; matrix products, arithmetic and copies ran while one was open for 4% -> 6% of each run, Pallas kernels for 0% -> 0%
where the time goes in v1:
time: 606 us; the launch traced here: 598 us
  waiting for transfers between devices  409 us (67%)
  other arithmetic  57.8 us (10%)
  matrix products  55.6 us (9%)
  local copies, waits for them, and re-layouts  51.1 us (8%)
  between operations  14.9 us (2%)
  starting transfers between devices  6.55 us (1%)
    reduce_scatter x1, waiting for transfers between devices, on_device(): lax.psum_scatter(jnp.einsum('icj,ick->jck', panel_part, left_side, prefer...  153 us
    psum x1, waiting for transfers between devices, on_device(): summed = lax.psum(grad_part, ('ia', 'ja'))  98.8 us
    ppermute x2, waiting for transfers between devices, on_device(): from_left = lax.ppermute(from_left, 'ia', ahead)  93 us
    psum x1, waiting for transfers between devices, on_device(): normed_grad = lax.psum(input_part, 'col')  32.2 us
    all_gather x1, waiting for transfers between devices, on_device(): row_panel = lax.all_gather(product_grad, 'ja', axis=2, tiled=True)  32 us
    another operation x2, other arithmetic, on_device(): proj_grads = jnp.stack([lin_a, gate_a, lin_b, gate_b]).astype(jnp.bfloat16)  22.7 us
    dot_general x1, local copies, waits for them, and re-layouts, on_device(): jnp.einsum('icj,ick->jck', panel_part, left_side, preferred_element_type=...  16.6 us
    dot_general x1, matrix products, on_device(): jnp.einsum('icj,ick->jck', panel_part, left_side, preferred_element_type=...  14.1 us
  transfers between devices with their start and end apart: 7, of which 6 were waited for; matrix products, arithmetic and copies ran while one was open for 6% of the time, Pallas kernels for 0%

profile of v1, /device:TPU:0, one launch (start us, length us, event | category | flops | bytes accessed | tf_op | source)
XLA Modules:
  0.0 597.8 jit_solution(7024431213077011554)
XLA Ops:
  7.2 0.0 copy-start
  7.2 0.0 all-gather.2.cloned.1.call-start
  7.2 4.3 copy.9
  11.5 0.0 all-gather.2.cloned.1.call-update
  11.5 0.0 reduce-scatter.2.cloned.1.call-start
  11.6 0.1 fusion.55
  11.7 0.1 broadcast_multiply_fusion.1
  11.8 3.5 convert_reduce_fusion
  15.3 4.8 fusion.10
  20.2 4.7 convolution_bitcast_fusion
  24.9 5.9 copy-done.1
  30.8 1.3 multiply_convert_fusion.5
  32.1 3.0 collective-permute-start.1
  35.1 46.7 %collective-permute-done.1 = bf16[128,64,128]{2,1,0:T(8,128)(2,1)} collective-permute-done((bf16[128,64,128]{2,1,0:T(8,128)(2,1)S(1)}, bf16[128,64,128]{2,1,0:T(8,128)(2,1)}, u32[]{:S(2)}, u32[]{:S(2)}) %collective-permute-start.1) | collective-permute-done | bytes 2097184 | tf_op jit(solution)/shard_map/ppermute | solution.py:46
  81.8 0.8 collective-permute-start.2
  82.6 2.6 collective-permute-start
  85.1 46.3 %collective-permute-done.2 = bf16[128,64,128]{2,1,0:T(8,128)(2,1)} collective-permute-done((bf16[128,64,128]{2,1,0:T(8,128)(2,1)}, bf16[128,64,128]{2,1,0:T(8,128)(2,1)}, u32[]{:S(2)}, u32[]{:S(2)}) %collective-permute-start.2) | collective-permute-done | bytes 2097184 | tf_op jit(solution)/shard_map/ppermute | solution.py:46
  131.5 32.0 %all-gather.2.cloned.1.call-done = bf16[128,64,512]{2,0,1:T(8,128)(2,1)} async-done(((bf16[128,64,128]{2,0,1:T(8,128)(2,1)}), bf16[128,64,512]{2,0,1:T(8,128)(2,1)}) %all-gather.2.cloned.1.call-update) | async-done | bytes 8388624 | tf_op jit(solution)/shard_map/all_gather | solution.py:32
  163.5 6.3 %fusion.32 = f32[64,128,128]{2,1,0:T(8,128)} fusion(bf16[128,64,128]{2,1,0:T(8,128)(2,1)} %collective-permute-done.2, bf16[128,64,512]{2,0,1:T(8,128)(2,1)} %all-gather.2.cloned.1.call-done, s32[]{:T(128)S(6)} %select_n.38), kind=kOutput, calls=%fused_computation.47 | convolution fusion | flops 268435456 | bytes 8388612 | tf_op jit(solution)/shard_map/icj,jck->ick/dot_general | solution.py:57
  169.8 5.4 copy.17
  175.3 6.3 %fusion.36 = f32[64,128,128]{2,1,0:T(8,128)} fusion(bf16[128,64,128]{2,1,0:T(8,128)(2,1)} %collective-permute-done, bf16[128,64,512]{2,0,1:T(8,128)(2,1)} %all-gather.2.cloned.1.call-done, s32[]{:T(128)S(6)} %select_n.34), kind=kOutput, calls=%fused_computation.51 | convolution fusion | flops 268435456 | bytes 8388612 | tf_op jit(solution)/shard_map/icj,jck->ick/dot_general | solution.py:49
  181.6 5.4 copy.13
  187.0 6.3 %fusion.34 = f32[64,128,128]{2,1,0:T(8,128)} fusion(bf16[128,64,128]{2,1,0:T(8,128)(2,1)} %collective-permute-done.1, bf16[128,64,512]{2,0,1:T(8,128)(2,1)} %all-gather.2.cloned.1.call-done, s32[]{:T(128)S(6)} %select_n.36), kind=kOutput, calls=%fused_computation.49 | convolution fusion | flops 268435456 | bytes 8388612 | tf_op jit(solution)/shard_map/icj,jck->ick/dot_general | solution.py:57
  193.3 5.4 copy.15
  198.7 5.7 fusion.38
  204.4 5.4 copy.12
  209.8 12.3 %fusion.26 = (bf16[1,128,64,128]{3,2,1,0:T(8,128)(2,1)S(1)}, f32[128,64,128]{2,1,0:T(8,128)}, bf16[128,64,128]{2,1,0:T(8,128)(2,1)S(1)}) fusion(f32[4,128,64,128]{3,2,0,1:T(8,128)} %copy-done.1, f32[128,128]{1,0:T(8,128)S(1)} %broadcast_multiply_fusion.1, f32[64,128,128]{1,0,2:T(8,128)} %copy.17, f32[64,128,128]{1,0,2:T(8,128)} %copy.15, ...), kind=kLoop, calls=%fused_computation.41 | loop fusion | flops 12582912 | bytes 33619968 | tf_op jit(solution)/shard_map/stack | solution.py:75
  222.1 14.1 %fusion.30 = f32[64,128,512]{2,1,0:T(8,128)} fusion(bf16[128,64,512]{2,0,1:T(8,128)(2,1)} %all-gather.2.cloned.1.call-done, bf16[128,64,128]{2,1,0:T(8,128)(2,1)S(1)} %get-tuple-element.8), kind=kOutput, calls=%fused_computation.45 | convolution fusion | flops 1073741824 | bytes 27262976 | tf_op jit(solution)/shard_map/icj,ick->jck/dot_general | solution.py:68
  236.3 16.6 %copy.20 = f32[64,128,512]{1,0,2:T(8,128)} copy(f32[64,128,512]{2,1,0:T(8,128)} %fusion.30) | data formatting | bytes 33554432 | tf_op jit(solution)/shard_map/icj,ick->jck/dot_general | solution.py:68
  252.8 0.0 reduce-scatter.2.cloned.1.call-update
  252.8 0.0 all-reduce.5.cloned.1.call-start
  252.9 152.7 %reduce-scatter.2.cloned.1.call-done = f32[128,64,128]{2,1,0:T(8,128)} async-done(((f32[512,64,128]{2,1,0:T(8,128)}), f32[128,64,128]{2,1,0:T(8,128)}) %reduce-scatter.2.cloned.1.call-update) | async-done | bytes 4194320 | tf_op jit(solution)/shard_map/reduce_scatter | solution.py:67
  405.6 10.3 %fusion.28 = (bf16[1,128,64,128]{3,2,1,0:T(8,128)(2,1)S(1)}, bf16[1,128,64,128]{3,2,1,0:T(8,128)(2,1)S(1)}, bf16[1,128,64,128]{3,2,1,0:T(8,128)(2,1)S(1)}) fusion(f32[128,64,128]{2,1,0:T(8,128)} %reduce-scatter.2.cloned.1.call-done, f32[128,128]{1,0:T(8,128)S(1)} %broadcast_multiply_fusion.1, f32[4,128,64,128]{3,2,0,1:T(8,128)} %copy-done.1, ...), kind=kLoop, calls=%fused_computation.43 | loop fusion | flops 19922944 | bytes 31522816 | tf_op jit(solution)/shard_map/stack | solution.py:75
  415.9 1.3 copy-done.6
  417.3 0.7 copy-done.7
  417.9 0.7 copy-done.8
  418.6 5.4 fusion.44
  424.0 0.0 all-reduce.5.cloned.1.call-update
  424.0 0.0 all-reduce.3.cloned.1.call-start
  424.1 6.7 %convolution_bitcast_fusion.1 = f32[128,128,128]{2,1,0:T(8,128)} fusion(bf16[1,128,64,128]{3,2,1,0:T(8,128)(2,1)} %copy-done.7, bf16[1,128,64,128]{3,2,1,0:T(8,128)(2,1)} %copy-done.6, bf16[1,128,64,128]{3,2,1,0:T(8,128)(2,1)} %copy-done.8, bf16[1,128,64,128]{3,2,1,0:T(8,128)(2,1)S(1)} %get-tuple-element.4, bf16[4,128,64]{1,2,0:T(8,128)(2,1)S(1)} %copy-done), kind=kOutput, calls=%fused_computation.40 | convolution fusion | flops 1086324736 | bytes 16842752 | tf_op jit(solution)/shard_map/wick,wdc->ikd/dot_general | solution.py:77
  430.8 0.0 all-reduce.3.cloned.1.call-update
  430.8 98.8 %all-reduce.5.cloned.1.call-done = f32[4,128,64]{1,2,0:T(8,128)} async-done(((f32[4,128,64]{1,2,0:T(8,128)}), f32[4,128,64]{1,2,0:T(8,128)}) %all-reduce.5.cloned.1.call-update) | async-done | bytes 131088 | tf_op jit(solution)/shard_map/psum | solution.py:87
  529.6 1.5 multiply_reduce_fusion.1
  531.1 3.1 psum.23
  534.9 1.6 broadcast_multiply_fusion
  536.5 32.2 %all-reduce.3.cloned.1.call-done = f32[128,128,128]{2,1,0:T(8,128)} async-done(((f32[128,128,128]{2,1,0:T(8,128)}), f32[128,128,128]{2,1,0:T(8,128)}) %all-reduce.3.cloned.1.call-update) | async-done | bytes 8388624 | tf_op jit(solution)/shard_map/psum | solution.py:80
  568.6 11.6 %multiply_reduce_fusion = (f32[128,128]{1,0:T(8,128)S(1)}, f32[128,128]{1,0:T(8,128)S(1)}) fusion(f32[128,128,128]{2,1,0:T(8,128)} %all-reduce.3.cloned.1.call-done, f32[128]{0:T(128)S(1)} %copy-done.9, f32[128,128]{1,0:T(8,128)S(1)} %add_rsqrt_fusion, f32[128,128]{1,0:T(8,128)S(1)} %broadcast_multiply_fusion.4, bf16[128,128,128]{2,1,0:T(8,128)(2,1)} %param.5), kind=kLoop, calls=%fused_computation.15 | loop fusion | flops 14647296 | bytes 12845568 | tf_op jit(solution)/shard_map/reduce_sum | solution.py:84
  580.3 10.7 %fusion.9 = bf16[128,128,128]{2,1,0:T(8,128)(2,1)} fusion(bf16[128,128,128]{2,1,0:T(8,128)(2,1)S(1)} %copy-done.4, f32[128,128,128]{2,1,0:T(8,128)S(1)} %copy-done.5, f32[128,128]{1,0:T(8,128)S(1)} %get-tuple-element.12, f32[128,128]{1,0:T(8,128)S(1)} %get-tuple-element.13, f32[128]{0:T(128)S(1)} %copy-done.9, f32[128,128]{1,0:T(8,128)S(1)} %add_rsqrt_fusion, ...), kind=kLoop, calls=%fused_computation.12 | loop fusion | flops 18874368 | bytes 17039872 | tf_op jit(solution)/shard_map/convert_element_type | solution.py:91
  (22 shorter events, 0.1 us)
Async XLA Ops:
  7.2 13.0 %copy-start = (bf16[4,128,64]{1,2,0:T(8,128)(2,1)S(1)}, bf16[4,128,64]{1,2,0:T(8,128)(2,1)}, u32[]{:S(2)}) copy-start(bf16[4,128,64]{1,2,0:T(8,128)(2,1)} %param.7) | copy-start | bytes 196612
  7.2 4.4 copy-start.10
  7.2 156.3 %all-gather.2.cloned.1.call-start = ((), (), s32[]{:S(2)}) async-start(), calls=%async_computation.1 | async-start | bytes 10485760 | tf_op jit(solution)/shard_map/all_gather | solution.py:32
  11.5 394.0 %reduce-scatter.2.cloned.1.call-start = ((), (), s32[]{:S(2)}) async-start(), calls=%async_computation.2 | async-start | bytes 20971520 | tf_op jit(solution)/shard_map/reduce_scatter | solution.py:67
  11.6 3.7 copy-start.2
  11.8 8.4 %copy-start.9 = (f32[128]{0:T(128)S(1)}, f32[128]{0:T(128)}, u32[]{:S(2)}) copy-start(f32[128]{0:T(128)} %param.6) | copy-start | bytes 1540
  24.9 5.9 copy-start.1
  32.1 49.7 %collective-permute-start.1 = (bf16[128,64,128]{2,1,0:T(8,128)(2,1)S(1)}, bf16[128,64,128]{2,1,0:T(8,128)(2,1)}, u32[]{:S(2)}, u32[]{:S(2)}) collective-permute-start(bf16[128,64,128]{2,1,0:T(8,128)(2,1)S(1)} %multiply_convert_fusion.5), channel_id=1, source_target_pairs={{0,8},{8,16},{16,24},{24,0},{1,9},{9,17},{17,25},{25,1},{2,10},{10... | collective-permute-start | bytes 6291464 | tf_op jit(solution)/shard_map/ppermute | solution.py:46
  81.8 49.7 %collective-permute-start.2 = (bf16[128,64,128]{2,1,0:T(8,128)(2,1)}, bf16[128,64,128]{2,1,0:T(8,128)(2,1)}, u32[]{:S(2)}, u32[]{:S(2)}) collective-permute-start(bf16[128,64,128]{2,1,0:T(8,128)(2,1)} %collective-permute-done.1), channel_id=1, source_target_pairs={{0,8},{8,16},{16,24},{24,0},{1,9},{9,17},{17,25},{25,1},{2,10},{10... | collective-permute-start | bytes 6291464 | tf_op jit(solution)/shard_map/ppermute | solution.py:46
  82.6 92.7 %collective-permute-start = (bf16[128,64,128]{2,1,0:T(8,128)(2,1)S(1)}, bf16[128,64,128]{2,1,0:T(8,128)(2,1)}, u32[]{:S(2)}, u32[]{:S(2)}) collective-permute-start(bf16[128,64,128]{2,1,0:T(8,128)(2,1)S(1)} %multiply_convert_fusion.5), channel_id=1, source_target_pairs={{0,24},{8,0},{16,8},{24,16},{1,25},{9,1},{17,9},{25,17},{2,26},{10... | collective-permute-start | bytes 6291464 | tf_op jit(solution)/shard_map/ppermute | solution.py:48
  252.8 276.7 %all-reduce.5.cloned.1.call-start = ((), (), s32[]{:S(2)}) async-start(), calls=%async_computation.4 | async-start | bytes 262144 | tf_op jit(solution)/shard_map/psum | solution.py:87
  405.5 13.0 %copy-start.3 = (bf16[128,128,128]{2,1,0:T(8,128)(2,1)S(1)}, bf16[128,128,128]{2,1,0:T(8,128)(2,1)}, u32[]{:S(2)}) copy-start(bf16[128,128,128]{2,1,0:T(8,128)(2,1)} %param.5) | copy-start | bytes 12582916
  415.9 1.4 copy-start.6
  415.9 2.0 copy-start.7
  415.9 2.7 copy-start.8
  424.0 144.6 %all-reduce.3.cloned.1.call-start = ((), (), s32[]{:S(2)}) async-start(), calls=%async_computation.3 | async-start | bytes 16777216 | tf_op jit(solution)/shard_map/psum | solution.py:80
  568.6 11.6 %copy-start.4 = (bf16[128,128,128]{2,1,0:T(8,128)(2,1)S(1)}, bf16[128,128,128]{2,1,0:T(8,128)(2,1)}, u32[]{:S(2)}) copy-start(bf16[128,128,128]{2,1,0:T(8,128)(2,1)} %param.5) | copy-start | bytes 12582916
  568.6 11.6 %copy-start.5 = (f32[128,128,128]{2,1,0:T(8,128)S(1)}, f32[128,128,128]{2,1,0:T(8,128)}, u32[]{:S(2)}) copy-start(f32[128,128,128]{2,1,0:T(8,128)} %all-reduce.3.cloned.1.call-done) | copy-start | bytes 25165828
Sparse Core Ops, SparseCore 0:
  11.6 151.8 all-gather.1
  253.0 152.5 reduce-scatter.1
  424.2 105.3 all-reduce.4
  531.9 36.6 all-reduce.2
